TPU v7x, 32 devices: a whole 2x2x4 slice. The times are simulated.
32 devices in a mesh: gx: 4 (over y, x), gy: 2 (over core), gz: 4 (over z).
Axes of the slice: x: 2, y: 2, z: 4, core: 2. Of those that a mesh axis runs over, the one named last changes fastest.
Arguments:
- populations: float32 [2, 19, 16, 32, 512], P(None, None, 'gx', 'gy', 'gz'), may hold values from 0.01 to 0.2
- solid: int32 [16, 32, 512], P('gx', 'gy', 'gz'), may hold values 0 or 1
Outputs:
- read: float32 [2, 19, 16, 32, 512], P(None, None, 'gx', 'gy', 'gz')
All inputs are finite; a program needn't handle non-finite values. No bound on the sum of `solid` on one device may be relied on, other than what follows from the above.
Results may differ from a plain program's by a relative error of at most 0.0001.
Values sent between devices are 32-bit elements; how exact they have to be, the bound alone decides.
No kernel may reach another device: no remote copies, remote signals or barrier semaphores. Data moves between devices by JAX's collectives and lax.ppermute only.
A program may use at most 64 MiB of HBM per device.

v0:
```python
import functools

import jax
import jax.numpy as jnp
from jax import lax
from jax.experimental import pallas as pl
from jax.experimental.pallas import tpu as pltpu
from jax.sharding import PartitionSpec as P


VEL = [
    (0, 0, 0),
    (1, 0, 0), (-1, 0, 0), (0, 1, 0), (0, -1, 0), (0, 0, 1), (0, 0, -1),
    (1, 1, 0), (-1, -1, 0), (1, -1, 0), (-1, 1, 0),
    (1, 0, 1), (-1, 0, -1), (1, 0, -1), (-1, 0, 1),
    (0, 1, 1), (0, -1, -1), (0, 1, -1), (0, -1, 1),
]
WEIGHT = [1.0 / 3.0] + [1.0 / 18.0] * 6 + [1.0 / 36.0] * 12
OPP = [0, 2, 1, 4, 3, 6, 5, 8, 7, 10, 9, 12, 11, 14, 13, 16, 15, 18, 17]
COUPLING = 0.9
TAU = (1.0, 0.8)
WALL = (0.3, 1.5)
W1, W2 = 1.0 / 18.0, 1.0 / 36.0
BLOCKED = 1e32
LIMIT = 1e29

XP = [i for i in range(19) if VEL[i][0] == 1]
XM = [i for i in range(19) if VEL[i][0] == -1]
ZP = [i for i in range(19) if VEL[i][2] == 1]
ZM = [i for i in range(19) if VEL[i][2] == -1]
YP = [i for i in range(19) if VEL[i][1] == 1]
YPAIR = [(i, VEL.index((VEL[i][0], -1, VEL[i][2]))) for i in YP]


def mirror(i):
    return VEL.index((VEL[i][0], VEL[i][1], -VEL[i][2]))


HALO = 12


def lanes(shape):
    return lax.broadcasted_iota(jnp.int32, shape, len(shape) - 1)


def roll(v, shift, axis):
    shift = shift % v.shape[axis]
    return pltpu.roll(v, shift, axis) if shift else v


def up(v):
    return roll(v, -1, 0)


def down(v):
    return roll(v, 1, 0)


def fold(v, rows):
    tile = lax.broadcasted_iota(jnp.int32, (8, v.shape[1]), 0)
    return jnp.where(tile < 4, v[:8], v[rows - 8 : rows])


def put(sheet, value, source, target):
    return jnp.where(lanes(sheet.shape) == target, roll(value, target - source, 1), sheet)


def y_index(nx):
    wide, mid = nx + 4, nx + 2
    psi = lambda k, x: k * wide + x + 2
    com = lambda a, x: 2 * wide + a * mid + x + 1
    base = 2 * wide + 3 * mid
    pair = lambda j, x: base + j * nx + x
    low, high = base + 5 * nx, base + 5 * nx + 1
    return psi, com, pair, low, high, high + 1


def first_kernel(pop_hbm, solid_hbm, field, face_high, face_low, rim_high, rim_low, pop, solid, sems):
    nx, ny, nz = solid_hbm.shape
    wide = nx + 4

    def face_side(step, dirs, edge, inner, face_out, rim_out):
        face = [field[f, edge] for f in range(5)] + [pop[1, i, edge] for i in dirs] + [field[f, inner] for f in range(2)]
        rim = jnp.zeros((ny, nz), jnp.float32)
        for cz, z_dirs, z_edge, z_inner in ((1, ZP, nz - 1, nz - 2), (-1, ZM, 0, 1)):
            near, far = rim_lanes(wide, step, cz)
            for k in range(2):
                for f, lane in ((k, z_edge), (10 + k, z_inner)):
                    rim = put(rim, face[k], lane, f * wide + near)
                    rim = put(rim, face[10 + k], lane, f * wide + far)
            for a in range(3):
                rim = put(rim, face[2 + a], z_edge, (2 + a) * wide + near)
            i = VEL.index((step, 0, cz))
            rim = put(rim, face[5 + dirs.index(i)], z_edge, (5 + z_dirs.index(i)) * wide + near)
        for f in range(HALO):
            face_out[f] = face[f]
        rim_out[...] = rim

    flag_copy = pltpu.make_async_copy(solid_hbm, solid, sems.at[nx])
    copies = [pltpu.make_async_copy(pop_hbm.at[:, :, x], pop.at[:, :, x], sems.at[x]) for x in range(nx)]
    flag_copy.start()
    for x in range(nx):
        copies[x].start()
    flag_copy.wait()
    for x in range(nx):
        copies[x].wait()
        fluid = solid[x] == 0
        q = []
        rho0 = rho1 = None
        for i in range(19):
            p0, p1 = pop[0, i, x], pop[1, i, x]
            rho0 = p0 if rho0 is None else rho0 + p0
            rho1 = p1 if rho1 is None else rho1 + p1
            q.append(p0 * (1.0 / TAU[0]) + p1 * (1.0 / TAU[1]))
        inverse = 1.0 / (rho0 * (1.0 / TAU[0]) + rho1 * (1.0 / TAU[1]))
        field[0, x] = jnp.where(fluid, rho0, -WALL[0])
        field[1, x] = jnp.where(fluid, rho1, -WALL[1])
        for a in range(3):
            total = None
            for i in range(1, 19):
                if VEL[i][a] == 1:
                    term = q[i] - q[OPP[i]]
                    total = term if total is None else total + term
            field[2 + a, x] = total * inverse
        if x == 1:
            face_side(-1, XM, 0, 1, face_low, rim_low)
    face_side(1, XP, nx - 1, nx - 2, face_high, rim_high)


def rim_lanes(wide, step, cz):
    if step == 1:
        return (1, 0) if cz == 1 else (3, 2)
    return (wide - 2, wide - 1) if cz == 1 else (wide - 4, wide - 3)


def column_kernel(field, pop, sheets):
    nx, ny, nz = field.shape[1:]
    wide = nx + 4
    for side, edge, inner, dirs in ((0, nz - 1, nz - 2, ZP), (1, 0, 1, ZM)):
        sheet = jnp.zeros((ny, nz), jnp.float32)
        for x in range(nx):
            for f in range(5):
                sheet = put(sheet, field[f, x], edge, f * wide + x + 2)
            for j, i in enumerate(dirs):
                sheet = put(sheet, pop[1, i, x], edge, (5 + j) * wide + x + 2)
            for k in range(2):
                sheet = put(sheet, field[k, x], inner, (10 + k) * wide + x + 2)
        sheets[side] = sheet


def join_kernel(nx, sheets, from_below, from_above, joined, rows_out):
    below, above = from_below[...], from_above[...]
    ny = below.shape[0]
    wide = nx + 4
    place = lax.rem(lanes(below.shape), wide)
    for side, shift in ((0, 0), (1, 2)):
        sheet = jnp.where(place < 2, roll(below, -shift, 1), sheets[side])
        sheet = jnp.where(place >= nx + 2, roll(above, shift, 1), sheet)
        joined[side] = sheet
        rows_out[side] = fold(sheet, ny)


def y_kernel(nx, field, pop, from_below, from_above, rows_out):
    psi, com, pair, low, high, _ = y_index(nx)
    below, above = (lambda f: from_below[f]), (lambda f: from_above[f])
    ny, nz = field.shape[2:]
    tile = lax.broadcasted_iota(jnp.int32, (8, nz), 0)
    for k in range(2):
        for x in range(nx):
            rows_out[psi(k, x)] = fold(field[k, x], ny)
        rows_out[psi(k, nx)], rows_out[psi(k, -1)] = fold(above(k), ny), fold(below(k), ny)
        rows_out[psi(k, nx + 1)], rows_out[psi(k, -2)] = fold(above(10 + k), ny), fold(below(10 + k), ny)
    for a in range(3):
        for x in range(nx):
            rows_out[com(a, x)] = fold(field[2 + a, x], ny)
        rows_out[com(a, nx)], rows_out[com(a, -1)] = fold(above(2 + a), ny), fold(below(2 + a), ny)
    for j, (plus, minus) in enumerate(YPAIR):
        for x in range(nx):
            rows_out[pair(j, x)] = jnp.where(tile < 4, pop[1, minus, x, 0:8], pop[1, plus, x, ny - 8 : ny])
    for where, source, step, dirs in ((low, below, 1, XP), (high, above, -1, XM)):
        plus, minus = dirs.index(VEL.index((step, 1, 0))) + 5, dirs.index(VEL.index((step, -1, 0))) + 5
        rows_out[where] = jnp.where(tile < 4, source(minus)[:8], source(plus)[ny - 8 :])


def merge_rows(from_y, n):
    if len(from_y) == 1:
        return from_y[0][n]
    below, above = from_y[0][n], from_y[1][n]
    return jnp.where(lax.broadcasted_iota(jnp.int32, above.shape, 0) < 4, above, below)


def z_kernel(y_parts, joined, *rest):
    from_y, (send_high, send_low) = rest[:y_parts], rest[y_parts:]
    for side, send in ((0, send_high), (1, send_low)):
        send[...] = jnp.concatenate([joined[side], merge_rows(from_y, side)], axis=0)


def store_rows(ref, at, main, halo):
    ny = main.shape[0]
    ref[(*at, slice(0, 8))] = halo
    ref[(*at, slice(8, 8 + ny))] = main
    ref[(*at, slice(8 + ny, 16 + ny))] = halo


def load_rows(ref, at, step, ny):
    main = ref[(*at, slice(8 + step, 8 + step + ny))]
    first = step if step >= 0 else 8 + ny + step
    return jnp.concatenate([main, ref[(*at, slice(first, first + 8))]], axis=0)


def posts(k, rho, vel, fluid, dirs, pop):
    out, made, parts = {}, {}, {}
    scaled = rho if TAU[k] == 1.0 else rho * (1.0 / TAU[k])
    square = vel[0] * vel[0] + vel[1] * vel[1] + vel[2] * vel[2]
    base = jnp.where(fluid, scaled - (1.5 * scaled) * square, BLOCKED)
    for weight in (W1, W2):
        parts[weight] = weight * base, (4.5 * weight) * scaled
    for i in dirs:
        whole, value = pop(i)
        cut = (lambda v: v) if whole else (lambda v: v[: value.shape[0]])
        if i == 0:
            equil = cut(base) * WEIGHT[0]
        else:
            lead = next(a for a in range(3) if VEL[i][a])
            main = i if VEL[i][lead] == 1 else OPP[i]
            if main not in made:
                along = None
                for a in range(3):
                    c = VEL[main][a]
                    if c:
                        u = cut(vel[a])
                        along = u if along is None else (along + u if c == 1 else along - u)
                share, factor = parts[WEIGHT[i]]
                flow = cut(factor) * along
                made[main] = cut(share) + flow * along, (2.0 / 3.0) * flow
            even, odd = made[main]
            equil = even + odd if main == i else even - odd
        out[i] = equil if TAU[k] == 1.0 else equil + (1.0 - 1.0 / TAU[k]) * value
    return out


def last_kernel(nx, y_parts, pop, solid, field, own_high, own_low, from_below, from_above, z_low, z_high, *rest):
    from_y, (out_hbm, out, a_ref, t_ref, dy_ref, dz_ref, zs_ref, gy_ref, gz_ref, post_ref, edge_ref, sems) = (
        rest[:y_parts],
        rest[y_parts:],
    )
    psi, com, pair, low, high, _ = y_index(nx)
    wide = nx + 4
    ny, nz = field.shape[2:]
    rows = lambda n: merge_rows(from_y, n)
    own_hi, own_lo, z_lo, z_hi = own_high[...], own_low[...], z_low[...], z_high[...]
    tall = (ny + 8, nz)
    lane = lanes(tall)

    def signed(k, x):
        if x < 0:
            main = from_below[k if x == -1 else 10 + k]
        elif x >= nx:
            main = from_above[k if x == nx else 10 + k]
        else:
            main = field[k, x]
        return jnp.concatenate([main, rows(psi(k, x))], axis=0)

    def shift_psi(k, x):
        at = (k, x + 2)
        a = jnp.abs(signed(k, x))
        column = k * wide + x + 2
        minus = jnp.where(lane == 0, jnp.abs(roll(z_lo, -column, 1)), roll(a, 1, 1))
        plus = jnp.where(lane == nz - 1, jnp.abs(roll(z_hi, nz - 1 - column, 1)), roll(a, -1, 1))
        z_sum, dz = plus + minus, plus - minus
        store_rows(a_ref, at, a[:ny], a[ny:])
        a_up, a_down = load_rows(a_ref, at, 1, ny), load_rows(a_ref, at, -1, ny)
        dy = a_up - a_down
        t_ref[at] = (a + a) + ((a_up + a_down) + z_sum)
        dy_ref[at] = dy
        dz_ref[at] = dz
        if -2 < x < nx + 1:
            store_rows(zs_ref, at, z_sum[:ny], z_sum[ny:])
            gy_ref[k, x + 1] = (dy + dy) + (load_rows(zs_ref, at, 1, ny) - load_rows(zs_ref, at, -1, ny))
            store_rows(a_ref, at, dz[:ny], dz[ny:])
            gz_ref[k, x + 1] = (dz + dz) + (load_rows(a_ref, at, 1, ny) + load_rows(a_ref, at, -1, ny))

    def speed(k, common, gradient):
        return [common[a] - (COUPLING * TAU[k] * W2) * gradient[a] for a in range(3)]

    def collide(k, x):
        n, other = x + 1, 1 - k
        gradient = (
            t_ref[other, n + 2] - t_ref[other, n],
            gy_ref[other, n] + (dy_ref[other, n + 2] + dy_ref[other, n]),
            gz_ref[other, n] + (dz_ref[other, n + 2] + dz_ref[other, n]),
        )
        common = []
        for a in range(3):
            main = from_below[2 + a] if x < 0 else from_above[2 + a] if x == nx else field[2 + a, x]
            common.append(jnp.concatenate([main, rows(com(a, x))], axis=0))
        own = signed(k, x)

        def population(i):
            if x < 0:
                main = from_below[5 + XP.index(i)]
            elif x == nx:
                main = from_above[5 + XM.index(i)]
            else:
                main = pop[1, i, x]
            if not VEL[i][1]:
                return False, main
            j = next(j for j, both in enumerate(YPAIR) if i in both)
            return True, jnp.concatenate([main, rows(low if x < 0 else high if x == nx else pair(j, x))], axis=0)

        dirs = XP if x < 0 else XM if x == nx else range(19)
        for i, value in posts(k, jnp.abs(own), speed(k, common, gradient), own > 0.0, dirs, population).items():
            if VEL[i][1]:
                store_rows(post_ref, (k, i, n), value[:ny], value[ny:])
            else:
                post_ref[k, i, n, 8 : 8 + ny] = value

    half = nz // 2

    def collide_sheets(k):
        is_low = lane < half
        part = lambda one, f, two, g: jnp.where(is_low, roll(one, -f * wide, 1), roll(two, half - g * wide, 1))
        right, left = (lambda v: roll(v, -1, 1)), (lambda v: roll(v, 1, 1))
        other = 1 - k
        own, a = part(z_lo, k, z_hi, k), jnp.abs(part(z_lo, other, z_hi, other))
        plus = jnp.abs(part(own_lo, other, own_hi, other))
        minus = jnp.abs(part(z_lo, 10 + other, z_hi, 10 + other))
        a_up, a_down = up(a), down(a)
        z_sum, dz, dy = plus + minus, plus - minus, a_up - a_down
        t = (a + a) + (a_up + a_down + z_sum)
        gradient = (
            right(t) - left(t),
            (dy + dy) + (up(z_sum) - down(z_sum) + right(dy) + left(dy)),
            (dz + dz) + (up(dz) + down(dz) + right(dz) + left(dz)),
        )
        common = [part(z_lo, 2 + a, z_hi, 2 + a) for a in range(3)]
        common[2] = jnp.where(is_low, common[2], -common[2])
        population = lambda i: (True, part(z_lo, 5 + ZP.index(i), z_hi, 5 + ZM.index(mirror(i))) if k else None)
        for i, value in posts(k, jnp.abs(own), speed(k, common, gradient), own > 0.0, ZP, population).items():
            edge_ref[k, ZP.index(i)] = roll(value, VEL[i][1], 0)[:ny]

    lane_of = lanes((ny, nz))

    def write(k, x):
        return pltpu.make_async_copy(out.at[k, :, x], out_hbm.at[k, :, x], sems.at[k, x])

    def finish(k, x):
        fluid = solid[x] == 0
        for i in range(19):
            cx, cy, cz = VEL[i]
            source = x - cx
            value = post_ref[k, i, source + 1, 8 - cy : 8 - cy + ny]
            if cz == 1:
                edge = roll(edge_ref[k, ZP.index(i)], -(source + 2), 1)
                value = jnp.where(lane_of == 0, edge, roll(value, 1, 1))
            elif cz == -1:
                edge = roll(edge_ref[k, ZP.index(mirror(i))], nz - 1 - half - (source + 2), 1)
                value = jnp.where(lane_of == nz - 1, edge, roll(value, -1, 1))
            if i:
                value = jnp.where(value < LIMIT, value, post_ref[k, OPP[i], x + 1, 8 : 8 + ny])
            out[k, i, x] = jnp.where(fluid, value, pop[k, i, x])
        write(k, x).start()

    for x in range(-2, 4):
        shift_psi(1, x)
    collide_sheets(0)
    for x in range(-1, 2):
        collide(0, x)
    later = [functools.partial(shift_psi, 0, x) for x in range(-2, nx + 2)]
    later += [functools.partial(collide_sheets, 1)] + [functools.partial(collide, 1, x) for x in range(-1, 2)]
    share = -(-len(later) // nx)
    for x in range(nx):
        if x + 4 < nx + 2:
            shift_psi(1, x + 4)
        if x + 2 < nx + 1:
            collide(0, x + 2)
        finish(0, x)
        for task in later[x * share : (x + 1) * share]:
            task()
    for x in range(nx):
        if x + 2 < nx + 1:
            collide(1, x + 2)
        finish(1, x)
    for k in range(2):
        for x in range(nx):
            write(k, x).wait()


def ring(value, axis, count, step):
    return lax.ppermute(value, axis, [(i, (i + step) % count) for i in range(count)])


def spread(high, low, axis, count):
    return ring(high, axis, count, 1), ring(low, axis, count, -1)


def spread_rows(rows, count):
    return spread(rows, rows, "gy", count) if count > 2 else (ring(rows, "gy", count, 1),)


def call(kernel, out_shape, *args, scratch=(), hbm_in=0, hbm_out=0, flops=200000, limit=16 * 2**20):
    space = lambda n, held: [pl.BlockSpec(memory_space=pltpu.HBM if j < held else pltpu.VMEM) for j in range(n)]
    args = [pltpu.with_memory_space_constraint(v, pltpu.HBM) if j < hbm_in else v for j, v in enumerate(args)]
    return pl.pallas_call(
        kernel,
        out_shape=[jax.ShapeDtypeStruct(*(s if isinstance(s[-1], type) else (s, jnp.float32))) for s in out_shape],
        in_specs=space(len(args), hbm_in),
        out_specs=space(len(out_shape), hbm_out),
        scratch_shapes=list(scratch),
        compiler_params=pltpu.CompilerParams(vmem_limit_bytes=limit),
        cost_estimate=pl.CostEstimate(flops=flops, bytes_accessed=flops, transcendentals=0),
    )(*args)


def body(sizes, pop, solid):
    return step(sizes, pop, solid)


def step(sizes, pop, solid):
    nx, ny, nz = solid.shape
    count = y_index(nx)[-1]
    wide = nx + 4
    face, plane, tall, padded = (HALO, ny, nz), (ny, nz), (ny + 8, nz), (ny + 16, nz)
    gx, gy, gz = sizes["gx"], sizes["gy"], sizes["gz"]
    y_parts = 1 if gy == 2 else 2
    field, face_high, face_low, rim_high, rim_low, pop_v, solid_v = call(
        first_kernel,
        [(5, nx, ny, nz), face, face, plane, plane, pop.shape, (solid.shape, jnp.int32)],
        pop, solid,
        scratch=[pltpu.SemaphoreType.DMA((nx + 1,))],
        hbm_in=2,
    )
    rims = spread(rim_high, rim_low, "gx", gx)
    faces = spread(face_high, face_low, "gx", gx)
    (sheets,) = call(column_kernel, [(2,) + plane], field, pop_v)
    joined, ends = call(functools.partial(join_kernel, nx), [(2,) + plane, (2, 8, nz)], sheets, *rims)
    ends = spread_rows(ends, gy)
    own = call(functools.partial(z_kernel, y_parts), [tall, tall], joined, *ends)
    far = spread(*own, "gz", gz)
    (rows,) = call(functools.partial(y_kernel, nx), [(count, 8, nz)], field, pop_v, *faces)
    from_y = spread_rows(rows, gy)
    vmem = lambda *s: pltpu.VMEM(s, jnp.float32)
    (result,) = call(
        functools.partial(last_kernel, nx, y_parts),
        [pop.shape],
        pop_v, solid_v, field, *own, *faces, *far, *from_y,
        scratch=[vmem(*pop.shape), vmem(2, wide, *padded)]
        + [vmem(2, wide, *tall)] * 3
        + [vmem(2, wide, *padded)]
        + [vmem(2, nx + 2, *tall)] * 2
        + [vmem(2, 19, nx + 2, *padded), vmem(2, 5, ny, nz), pltpu.SemaphoreType.DMA((2, nx))],
        hbm_out=1,
    )
    return result


def solution(mesh):
    sizes = dict(mesh.shape)
    spec = P(None, None, "gx", "gy", "gz")
    return jax.shard_map(
        functools.partial(body, sizes),
        mesh=mesh,
        in_specs=(spec, P("gx", "gy", "gz")),
        out_specs=spec,
        check_vma=False,
    )
```

profile of v0, /device:TPU:0, one launch (start us, length us, event | category | flops | bytes accessed | tf_op | source)
XLA Modules:
  0.0 24.7 jit_solution(5391735900383025446)
XLA Ops:
  0.0 1.4 %shard_map.28 = (f32[5,4,16,128]{3,2,1,0:T(8,128)S(1)}, f32[12,16,128]{2,1,0:T(8,128)S(1)}, f32[12,16,128]{2,1,0:T(8,128)S(1)}, f32[16,128]{1,0:T(8,128)S(1)}, f...) custom-call(f32[2,19,4,16,128]{4,3,2,1,0:T(8,128)} %pop_hbm.1, ...), custom_call_target="tpu_custom_call" | custom-call | flops 200000 | bytes 200000 | tf_op jit(solution)/shard_map/pallas_call | solution.py:404
  1.5 3.0 %collective-permute-start.3 = (f32[12,16,128]{2,1,0:T(8,128)S(1)}, f32[12,16,128]{2,1,0:T(8,128)S(1)}, u32[]{:S(2)}, u32[]{:S(2)}) collective-permute-start(f32[12,16,128]{2,1,0:T(8,128)S(1)} %get-tuple-element.25), channel_id=1, source_target_pairs={{0,8},{8,16},{16,24},{24,0},{1,9},{9,17},{17,25},{25,1},{2,10},{10... | collective-permute-start | bytes 294920 | tf_op jit(solution)/shard_map/ppermute | solution.py:390
  4.5 1.0 %collective-permute-start.4 = (f32[12,16,128]{2,1,0:T(8,128)S(1)}, f32[12,16,128]{2,1,0:T(8,128)S(1)}, u32[]{:S(2)}, u32[]{:S(2)}) collective-permute-start(f32[12,16,128]{2,1,0:T(8,128)S(1)} %get-tuple-element.26), channel_id=1, source_target_pairs={{0,24},{8,0},{16,8},{24,16},{1,25},{9,1},{17,9},{25,17},{2,26},{10... | collective-permute-start | bytes 294920 | tf_op jit(solution)/shard_map/ppermute | solution.py:390
  5.5 3.4 %collective-permute-done.3.from_below = f32[12,16,128]{2,1,0:T(8,128)S(1)} collective-permute-done((f32[12,16,128]{2,1,0:T(8,128)S(1)}, f32[12,16,128]{2,1,0:T(8,128)S(1)}, u32[]{:S(2)}, u32[]{:S(2)}) %collective-permute-start.3) | collective-permute-done | bytes 98336 | tf_op jit(solution)/shard_map/ppermute | solution.py:390
  8.9 1.7 %collective-permute-done.4.from_above = f32[12,16,128]{2,1,0:T(8,128)S(1)} collective-permute-done((f32[12,16,128]{2,1,0:T(8,128)S(1)}, f32[12,16,128]{2,1,0:T(8,128)S(1)}, u32[]{:S(2)}, u32[]{:S(2)}) %collective-permute-start.4) | collective-permute-done | bytes 98336 | tf_op jit(solution)/shard_map/ppermute | solution.py:390
  10.6 0.1 collective-permute-start.7
  10.7 1.6 %collective-permute-start = (f32[16,128]{1,0:T(8,128)S(1)}, f32[16,128]{1,0:T(8,128)S(1)}, u32[]{:S(2)}, u32[]{:S(2)}) collective-permute-start(f32[16,128]{1,0:T(8,128)S(1)} %get-tuple-element.19), channel_id=1, source_target_pairs={{0,8},{8,16},{16,24},{24,0},{1,9},{9,17},{17,25},{25,1},{2,10},{10... | collective-permute-start | bytes 24584 | tf_op jit(solution)/shard_map/ppermute | solution.py:390
  12.3 1.4 %collective-permute-start.1 = (f32[16,128]{1,0:T(8,128)S(1)}, f32[16,128]{1,0:T(8,128)S(1)}, u32[]{:S(2)}, u32[]{:S(2)}) collective-permute-start(f32[16,128]{1,0:T(8,128)S(1)} %get-tuple-element.20), channel_id=1, source_target_pairs={{0,24},{8,0},{16,8},{24,16},{1,25},{9,1},{17,9},{25,17},{2,26},{10... | collective-permute-start | bytes 24584 | tf_op jit(solution)/shard_map/ppermute | solution.py:390
  13.7 0.3 %shard_map.29.sheets = f32[2,16,128]{2,1,0:T(8,128)S(1)} custom-call(f32[5,4,16,128]{3,2,1,0:T(8,128)S(1)} %get-tuple-element.18.field, f32[2,19,4,16,128]{4,3,2,1,0:T(8,128)S(1)} %get-tuple-element.16.pop), custom_call_target="tpu_custom_call" | custom-call | flops 200000 | bytes 200000 | tf_op jit(solution)/shard_map/pallas_call | solution.py:404
  13.9 1.4 %collective-permute-done.from_below = f32[16,128]{1,0:T(8,128)S(1)} collective-permute-done((f32[16,128]{1,0:T(8,128)S(1)}, f32[16,128]{1,0:T(8,128)S(1)}, u32[]{:S(2)}, u32[]{:S(2)}) %collective-permute-start) | collective-permute-done | bytes 8224 | tf_op jit(solution)/shard_map/ppermute | solution.py:390
  15.3 0.7 %collective-permute-done.1.from_above = f32[16,128]{1,0:T(8,128)S(1)} collective-permute-done((f32[16,128]{1,0:T(8,128)S(1)}, f32[16,128]{1,0:T(8,128)S(1)}, u32[]{:S(2)}, u32[]{:S(2)}) %collective-permute-start.1) | collective-permute-done | bytes 8224 | tf_op jit(solution)/shard_map/ppermute | solution.py:390
  16.0 0.1 shard_map.30
  16.0 0.0 collective-permute-start.2
  16.1 1.2 %collective-permute-done.2.rest_0_ = f32[2,8,128]{2,1,0:T(8,128)S(1)} collective-permute-done((f32[2,8,128]{2,1,0:T(8,128)S(1)}, f32[2,8,128]{2,1,0:T(8,128)S(1)}, u32[]{:S(2)}, u32[]{:S(2)}) %collective-permute-start.2) | collective-permute-done | bytes 8224 | tf_op jit(solution)/shard_map/ppermute | solution.py:390
  17.2 1.6 %collective-permute-start.5 = (f32[24,128]{1,0:T(8,128)S(1)}, f32[24,128]{1,0:T(8,128)S(1)}, u32[]{:S(2)}, u32[]{:S(2)}) collective-permute-start(f32[24,128]{1,0:T(8,128)S(1)} %get-tuple-element.23.own_high), channel_id=1, source_target_pairs={{0,1},{1,2},{2,3},{3,0},{4,5},{5,6},{6,7},{7,4},{8,9},{9,10},{10,1... | collective-permute-start | bytes 36872 | tf_op jit(solution)/shard_map/ppermute | solution.py:390
  18.8 2.2 %collective-permute-start.6 = (f32[24,128]{1,0:T(8,128)S(1)}, f32[24,128]{1,0:T(8,128)S(1)}, u32[]{:S(2)}, u32[]{:S(2)}) collective-permute-start(f32[24,128]{1,0:T(8,128)S(1)} %get-tuple-element.24.own_low), channel_id=1, source_target_pairs={{0,3},{1,0},{2,1},{3,2},{4,7},{5,4},{6,5},{7,6},{8,11},{9,8},{10,9... | collective-permute-start | bytes 36872 | tf_op jit(solution)/shard_map/ppermute | solution.py:390
  21.1 1.7 %collective-permute-done.5.z_low = f32[24,128]{1,0:T(8,128)S(1)} collective-permute-done((f32[24,128]{1,0:T(8,128)S(1)}, f32[24,128]{1,0:T(8,128)S(1)}, u32[]{:S(2)}, u32[]{:S(2)}) %collective-permute-start.5) | collective-permute-done | bytes 12320 | tf_op jit(solution)/shard_map/ppermute | solution.py:390
  22.7 0.0 collective-permute-done.6.z_high
  22.7 0.0 collective-permute-done.7.rest_0_
  22.7 2.0 %shard_map.33 = f32[2,19,4,16,128]{4,3,2,1,0:T(8,128)} custom-call(f32[2,19,4,16,128]{4,3,2,1,0:T(8,128)S(1)} %get-tuple-element.16.pop, s32[4,16,128]{2,1,0:T(8,128)S(1)} %get-tuple-element.17.solid, f32[5,4,16,128]{3,2,1,0:T(8,128)S(1)} %get-tuple-element.18.field, f32[24,128]{1,0:T(8,128)S(1)} %get-tuple-element.23.own_high, ...), custom_call_target="tpu_custom_call" | custom-call | flops 200000 | bytes 200000 | tf_op jit(solution)/shard_map/pallas_call | solution.py:404
  (2 shorter events, 0.0 us)
Async XLA Ops:
  1.5 7.4 %collective-permute-start.3 = (f32[12,16,128]{2,1,0:T(8,128)S(1)}, f32[12,16,128]{2,1,0:T(8,128)S(1)}, u32[]{:S(2)}, u32[]{:S(2)}) collective-permute-start(f32[12,16,128]{2,1,0:T(8,128)S(1)} %get-tuple-element.25), channel_id=1, source_target_pairs={{0,8},{8,16},{16,24},{24,0},{1,9},{9,17},{17,25},{25,1},{2,10},{10... | collective-permute-start | bytes 294920 | tf_op jit(solution)/shard_map/ppermute | solution.py:390
  4.5 6.1 %collective-permute-start.4 = (f32[12,16,128]{2,1,0:T(8,128)S(1)}, f32[12,16,128]{2,1,0:T(8,128)S(1)}, u32[]{:S(2)}, u32[]{:S(2)}) collective-permute-start(f32[12,16,128]{2,1,0:T(8,128)S(1)} %get-tuple-element.26), channel_id=1, source_target_pairs={{0,24},{8,0},{16,8},{24,16},{1,25},{9,1},{17,9},{25,17},{2,26},{10... | collective-permute-start | bytes 294920 | tf_op jit(solution)/shard_map/ppermute | solution.py:390
  10.6 12.1 %collective-permute-start.7 = (f32[56,8,128]{2,1,0:T(8,128)S(1)}, f32[56,8,128]{2,1,0:T(8,128)S(1)}, u32[]{:S(2)}, u32[]{:S(2)}) collective-permute-start(f32[56,8,128]{2,1,0:T(8,128)S(1)} %shard_map.32), channel_id=1, source_target_pairs={{0,4},{4,0},{1,5},{5,1},{2,6},{6,2},{3,7},{7,3},{8,12},{12,8},{9,1... | collective-permute-start | bytes 688136 | tf_op jit(solution)/shard_map/ppermute | solution.py:390
  10.7 4.6 %collective-permute-start = (f32[16,128]{1,0:T(8,128)S(1)}, f32[16,128]{1,0:T(8,128)S(1)}, u32[]{:S(2)}, u32[]{:S(2)}) collective-permute-start(f32[16,128]{1,0:T(8,128)S(1)} %get-tuple-element.19), channel_id=1, source_target_pairs={{0,8},{8,16},{16,24},{24,0},{1,9},{9,17},{17,25},{25,1},{2,10},{10... | collective-permute-start | bytes 24584 | tf_op jit(solution)/shard_map/ppermute | solution.py:390
  12.3 3.7 %collective-permute-start.1 = (f32[16,128]{1,0:T(8,128)S(1)}, f32[16,128]{1,0:T(8,128)S(1)}, u32[]{:S(2)}, u32[]{:S(2)}) collective-permute-start(f32[16,128]{1,0:T(8,128)S(1)} %get-tuple-element.20), channel_id=1, source_target_pairs={{0,24},{8,0},{16,8},{24,16},{1,25},{9,1},{17,9},{25,17},{2,26},{10... | collective-permute-start | bytes 24584 | tf_op jit(solution)/shard_map/ppermute | solution.py:390
  16.0 1.2 %collective-permute-start.2 = (f32[2,8,128]{2,1,0:T(8,128)S(1)}, f32[2,8,128]{2,1,0:T(8,128)S(1)}, u32[]{:S(2)}, u32[]{:S(2)}) collective-permute-start(f32[2,8,128]{2,1,0:T(8,128)S(1)} %get-tuple-element.22), channel_id=1, source_target_pairs={{0,4},{4,0},{1,5},{5,1},{2,6},{6,2},{3,7},{7,3},{8,12},{12,8},{9,1... | collective-permute-start | bytes 24584 | tf_op jit(solution)/shard_map/ppermute | solution.py:390
  17.2 5.5 %collective-permute-start.5 = (f32[24,128]{1,0:T(8,128)S(1)}, f32[24,128]{1,0:T(8,128)S(1)}, u32[]{:S(2)}, u32[]{:S(2)}) collective-permute-start(f32[24,128]{1,0:T(8,128)S(1)} %get-tuple-element.23.own_high), channel_id=1, source_target_pairs={{0,1},{1,2},{2,3},{3,0},{4,5},{5,6},{6,7},{7,4},{8,9},{9,10},{10,1... | collective-permute-start | bytes 36872 | tf_op jit(solution)/shard_map/ppermute | solution.py:390
  18.8 3.9 %collective-permute-start.6 = (f32[24,128]{1,0:T(8,128)S(1)}, f32[24,128]{1,0:T(8,128)S(1)}, u32[]{:S(2)}, u32[]{:S(2)}) collective-permute-start(f32[24,128]{1,0:T(8,128)S(1)} %get-tuple-element.24.own_low), channel_id=1, source_target_pairs={{0,3},{1,0},{2,1},{3,2},{4,7},{5,4},{6,5},{7,6},{8,11},{9,8},{10,9... | collective-permute-start | bytes 36872 | tf_op jit(solution)/shard_map/ppermute | solution.py:390
where the time goes:
time: 24.8 us; the launch traced here: 24.7 us
  starting transfers between devices  10.9 us (44%)
  waiting for transfers between devices  9.94 us (40%)
  Pallas kernels  3.77 us (15%)
    ppermute x8, starting transfers between devices, ring(): lax.ppermute(value, axis, [(i, (i + step) % count) for i in range(count)])  10.9 us
    ppermute x8, waiting for transfers between devices, ring(): lax.ppermute(value, axis, [(i, (i + step) % count) for i in range(count)])  9.94 us
    pallas_call x6, Pallas kernels, call(): pl.pallas_call(kernel, out_shape=[jax.ShapeDtypeStruct(*(s if isinstance(...  3.77 us
  transfers between devices with their start and end apart: 8, of which 6 were waited for; matrix products, arithmetic and copies ran while one was open for 0% of the time, Pallas kernels for 1%

commit v1 on v0

--- a/solution.py
+++ b/solution.py
@@ -342,7 +342,8 @@
     lane_of = lanes((ny, nz))
 
     def write(k, x):
-        return pltpu.make_async_copy(out.at[k, :, x], out_hbm.at[k, :, x], sems.at[k, x])
+        cut = (k, slice(None), slice(x - x % 2, min(x - x % 2 + 2, nx)))
+        return pltpu.make_async_copy(out.at[cut], out_hbm.at[cut], sems.at[k, x])
 
     def finish(k, x):
         fluid = solid[x] == 0
@@ -359,7 +360,8 @@
             if i:
                 value = jnp.where(value < LIMIT, value, post_ref[k, OPP[i], x + 1, 8 : 8 + ny])
             out[k, i, x] = jnp.where(fluid, value, pop[k, i, x])
-        write(k, x).start()
+        if x % 2 or x == nx - 1:
+            write(k, x).start()
 
     for x in range(-2, 4):
         shift_psi(1, x)
@@ -383,7 +385,8 @@
         finish(1, x)
     for k in range(2):
         for x in range(nx):
-            write(k, x).wait()
+            if x % 2 or x == nx - 1:
+                write(k, x).wait()
 
 
 def ring(value, axis, count, step):

time: 24.8 us -> 24.9 us (level)
  no operation moved by 1% of the time
where the time goes in v1:
time: 24.9 us; the launch traced here: 24.7 us
  starting transfers between devices  10.9 us (44%)
  waiting for transfers between devices  9.94 us (40%)
  Pallas kernels  3.84 us (15%)
    ppermute x8, starting transfers between devices, ring(): lax.ppermute(value, axis, [(i, (i + step) % count) for i in range(count)])  10.9 us
    ppermute x8, waiting for transfers between devices, ring(): lax.ppermute(value, axis, [(i, (i + step) % count) for i in range(count)])  9.94 us
    pallas_call x6, Pallas kernels, call(): pl.pallas_call(kernel, out_shape=[jax.ShapeDtypeStruct(*(s if isinstance(...  3.84 us
  transfers between devices with their start and end apart: 8, of which 6 were waited for; matrix products, arithmetic and copies ran while one was open for 0% of the time, Pallas kernels for 1%

profile of v1, /device:TPU:0, one launch (start us, length us, event | category | flops | bytes accessed | tf_op | source)
XLA Modules:
  0.0 24.7 jit_solution(12861082393183675211)
XLA Ops:
  0.0 1.4 %shard_map.28 = (f32[5,4,16,128]{3,2,1,0:T(8,128)S(1)}, f32[12,16,128]{2,1,0:T(8,128)S(1)}, f32[12,16,128]{2,1,0:T(8,128)S(1)}, f32[16,128]{1,0:T(8,128)S(1)}, f...) custom-call(f32[2,19,4,16,128]{4,3,2,1,0:T(8,128)} %pop_hbm.1, ...), custom_call_target="tpu_custom_call" | custom-call | flops 200000 | bytes 200000 | tf_op jit(solution)/shard_map/pallas_call | solution.py:407
  1.5 3.0 %collective-permute-start.3 = (f32[12,16,128]{2,1,0:T(8,128)S(1)}, f32[12,16,128]{2,1,0:T(8,128)S(1)}, u32[]{:S(2)}, u32[]{:S(2)}) collective-permute-start(f32[12,16,128]{2,1,0:T(8,128)S(1)} %get-tuple-element.25), channel_id=1, source_target_pairs={{0,8},{8,16},{16,24},{24,0},{1,9},{9,17},{17,25},{25,1},{2,10},{10... | collective-permute-start | bytes 294920 | tf_op jit(solution)/shard_map/ppermute | solution.py:393
  4.5 1.0 %collective-permute-start.4 = (f32[12,16,128]{2,1,0:T(8,128)S(1)}, f32[12,16,128]{2,1,0:T(8,128)S(1)}, u32[]{:S(2)}, u32[]{:S(2)}) collective-permute-start(f32[12,16,128]{2,1,0:T(8,128)S(1)} %get-tuple-element.26), channel_id=1, source_target_pairs={{0,24},{8,0},{16,8},{24,16},{1,25},{9,1},{17,9},{25,17},{2,26},{10... | collective-permute-start | bytes 294920 | tf_op jit(solution)/shard_map/ppermute | solution.py:393
  5.5 3.4 %collective-permute-done.3.from_below = f32[12,16,128]{2,1,0:T(8,128)S(1)} collective-permute-done((f32[12,16,128]{2,1,0:T(8,128)S(1)}, f32[12,16,128]{2,1,0:T(8,128)S(1)}, u32[]{:S(2)}, u32[]{:S(2)}) %collective-permute-start.3) | collective-permute-done | bytes 98336 | tf_op jit(solution)/shard_map/ppermute | solution.py:393
  8.9 1.7 %collective-permute-done.4.from_above = f32[12,16,128]{2,1,0:T(8,128)S(1)} collective-permute-done((f32[12,16,128]{2,1,0:T(8,128)S(1)}, f32[12,16,128]{2,1,0:T(8,128)S(1)}, u32[]{:S(2)}, u32[]{:S(2)}) %collective-permute-start.4) | collective-permute-done | bytes 98336 | tf_op jit(solution)/shard_map/ppermute | solution.py:393
  10.6 0.1 collective-permute-start.7
  10.7 1.6 %collective-permute-start = (f32[16,128]{1,0:T(8,128)S(1)}, f32[16,128]{1,0:T(8,128)S(1)}, u32[]{:S(2)}, u32[]{:S(2)}) collective-permute-start(f32[16,128]{1,0:T(8,128)S(1)} %get-tuple-element.19), channel_id=1, source_target_pairs={{0,8},{8,16},{16,24},{24,0},{1,9},{9,17},{17,25},{25,1},{2,10},{10... | collective-permute-start | bytes 24584 | tf_op jit(solution)/shard_map/ppermute | solution.py:393
  12.3 1.4 %collective-permute-start.1 = (f32[16,128]{1,0:T(8,128)S(1)}, f32[16,128]{1,0:T(8,128)S(1)}, u32[]{:S(2)}, u32[]{:S(2)}) collective-permute-start(f32[16,128]{1,0:T(8,128)S(1)} %get-tuple-element.20), channel_id=1, source_target_pairs={{0,24},{8,0},{16,8},{24,16},{1,25},{9,1},{17,9},{25,17},{2,26},{10... | collective-permute-start | bytes 24584 | tf_op jit(solution)/shard_map/ppermute | solution.py:393
  13.7 0.3 %shard_map.29.sheets = f32[2,16,128]{2,1,0:T(8,128)S(1)} custom-call(f32[5,4,16,128]{3,2,1,0:T(8,128)S(1)} %get-tuple-element.18.field, f32[2,19,4,16,128]{4,3,2,1,0:T(8,128)S(1)} %get-tuple-element.16.pop), custom_call_target="tpu_custom_call" | custom-call | flops 200000 | bytes 200000 | tf_op jit(solution)/shard_map/pallas_call | solution.py:407
  13.9 1.4 %collective-permute-done.from_below = f32[16,128]{1,0:T(8,128)S(1)} collective-permute-done((f32[16,128]{1,0:T(8,128)S(1)}, f32[16,128]{1,0:T(8,128)S(1)}, u32[]{:S(2)}, u32[]{:S(2)}) %collective-permute-start) | collective-permute-done | bytes 8224 | tf_op jit(solution)/shard_map/ppermute | solution.py:393
  15.3 0.7 %collective-permute-done.1.from_above = f32[16,128]{1,0:T(8,128)S(1)} collective-permute-done((f32[16,128]{1,0:T(8,128)S(1)}, f32[16,128]{1,0:T(8,128)S(1)}, u32[]{:S(2)}, u32[]{:S(2)}) %collective-permute-start.1) | collective-permute-done | bytes 8224 | tf_op jit(solution)/shard_map/ppermute | solution.py:393
  16.0 0.1 shard_map.30
  16.0 0.0 collective-permute-start.2
  16.1 1.2 %collective-permute-done.2.rest_0_ = f32[2,8,128]{2,1,0:T(8,128)S(1)} collective-permute-done((f32[2,8,128]{2,1,0:T(8,128)S(1)}, f32[2,8,128]{2,1,0:T(8,128)S(1)}, u32[]{:S(2)}, u32[]{:S(2)}) %collective-permute-start.2) | collective-permute-done | bytes 8224 | tf_op jit(solution)/shard_map/ppermute | solution.py:393
  17.2 1.6 %collective-permute-start.5 = (f32[24,128]{1,0:T(8,128)S(1)}, f32[24,128]{1,0:T(8,128)S(1)}, u32[]{:S(2)}, u32[]{:S(2)}) collective-permute-start(f32[24,128]{1,0:T(8,128)S(1)} %get-tuple-element.23.own_high), channel_id=1, source_target_pairs={{0,1},{1,2},{2,3},{3,0},{4,5},{5,6},{6,7},{7,4},{8,9},{9,10},{10,1... | collective-permute-start | bytes 36872 | tf_op jit(solution)/shard_map/ppermute | solution.py:393
  18.8 2.2 %collective-permute-start.6 = (f32[24,128]{1,0:T(8,128)S(1)}, f32[24,128]{1,0:T(8,128)S(1)}, u32[]{:S(2)}, u32[]{:S(2)}) collective-permute-start(f32[24,128]{1,0:T(8,128)S(1)} %get-tuple-element.24.own_low), channel_id=1, source_target_pairs={{0,3},{1,0},{2,1},{3,2},{4,7},{5,4},{6,5},{7,6},{8,11},{9,8},{10,9... | collective-permute-start | bytes 36872 | tf_op jit(solution)/shard_map/ppermute | solution.py:393
  21.1 1.7 %collective-permute-done.5.z_low = f32[24,128]{1,0:T(8,128)S(1)} collective-permute-done((f32[24,128]{1,0:T(8,128)S(1)}, f32[24,128]{1,0:T(8,128)S(1)}, u32[]{:S(2)}, u32[]{:S(2)}) %collective-permute-start.5) | collective-permute-done | bytes 12320 | tf_op jit(solution)/shard_map/ppermute | solution.py:393
  22.7 0.0 collective-permute-done.6.z_high
  22.7 0.0 collective-permute-done.7.rest_0_
  22.7 2.0 %shard_map.33 = f32[2,19,4,16,128]{4,3,2,1,0:T(8,128)} custom-call(f32[2,19,4,16,128]{4,3,2,1,0:T(8,128)S(1)} %get-tuple-element.16.pop, s32[4,16,128]{2,1,0:T(8,128)S(1)} %get-tuple-element.17.solid, f32[5,4,16,128]{3,2,1,0:T(8,128)S(1)} %get-tuple-element.18.field, f32[24,128]{1,0:T(8,128)S(1)} %get-tuple-element.23.own_high, ...), custom_call_target="tpu_custom_call" | custom-call | flops 200000 | bytes 200000 | tf_op jit(solution)/shard_map/pallas_call | solution.py:407
  (2 shorter events, 0.0 us)
Async XLA Ops:
  1.5 7.4 %collective-permute-start.3 = (f32[12,16,128]{2,1,0:T(8,128)S(1)}, f32[12,16,128]{2,1,0:T(8,128)S(1)}, u32[]{:S(2)}, u32[]{:S(2)}) collective-permute-start(f32[12,16,128]{2,1,0:T(8,128)S(1)} %get-tuple-element.25), channel_id=1, source_target_pairs={{0,8},{8,16},{16,24},{24,0},{1,9},{9,17},{17,25},{25,1},{2,10},{10... | collective-permute-start | bytes 294920 | tf_op jit(solution)/shard_map/ppermute | solution.py:393
  4.5 6.1 %collective-permute-start.4 = (f32[12,16,128]{2,1,0:T(8,128)S(1)}, f32[12,16,128]{2,1,0:T(8,128)S(1)}, u32[]{:S(2)}, u32[]{:S(2)}) collective-permute-start(f32[12,16,128]{2,1,0:T(8,128)S(1)} %get-tuple-element.26), channel_id=1, source_target_pairs={{0,24},{8,0},{16,8},{24,16},{1,25},{9,1},{17,9},{25,17},{2,26},{10... | collective-permute-start | bytes 294920 | tf_op jit(solution)/shard_map/ppermute | solution.py:393
  10.6 12.1 %collective-permute-start.7 = (f32[56,8,128]{2,1,0:T(8,128)S(1)}, f32[56,8,128]{2,1,0:T(8,128)S(1)}, u32[]{:S(2)}, u32[]{:S(2)}) collective-permute-start(f32[56,8,128]{2,1,0:T(8,128)S(1)} %shard_map.32), channel_id=1, source_target_pairs={{0,4},{4,0},{1,5},{5,1},{2,6},{6,2},{3,7},{7,3},{8,12},{12,8},{9,1... | collective-permute-start | bytes 688136 | tf_op jit(solution)/shard_map/ppermute | solution.py:393
  10.7 4.6 %collective-permute-start = (f32[16,128]{1,0:T(8,128)S(1)}, f32[16,128]{1,0:T(8,128)S(1)}, u32[]{:S(2)}, u32[]{:S(2)}) collective-permute-start(f32[16,128]{1,0:T(8,128)S(1)} %get-tuple-element.19), channel_id=1, source_target_pairs={{0,8},{8,16},{16,24},{24,0},{1,9},{9,17},{17,25},{25,1},{2,10},{10... | collective-permute-start | bytes 24584 | tf_op jit(solution)/shard_map/ppermute | solution.py:393
  12.3 3.7 %collective-permute-start.1 = (f32[16,128]{1,0:T(8,128)S(1)}, f32[16,128]{1,0:T(8,128)S(1)}, u32[]{:S(2)}, u32[]{:S(2)}) collective-permute-start(f32[16,128]{1,0:T(8,128)S(1)} %get-tuple-element.20), channel_id=1, source_target_pairs={{0,24},{8,0},{16,8},{24,16},{1,25},{9,1},{17,9},{25,17},{2,26},{10... | collective-permute-start | bytes 24584 | tf_op jit(solution)/shard_map/ppermute | solution.py:393
  16.0 1.2 %collective-permute-start.2 = (f32[2,8,128]{2,1,0:T(8,128)S(1)}, f32[2,8,128]{2,1,0:T(8,128)S(1)}, u32[]{:S(2)}, u32[]{:S(2)}) collective-permute-start(f32[2,8,128]{2,1,0:T(8,128)S(1)} %get-tuple-element.22), channel_id=1, source_target_pairs={{0,4},{4,0},{1,5},{5,1},{2,6},{6,2},{3,7},{7,3},{8,12},{12,8},{9,1... | collective-permute-start | bytes 24584 | tf_op jit(solution)/shard_map/ppermute | solution.py:393
  17.2 5.5 %collective-permute-start.5 = (f32[24,128]{1,0:T(8,128)S(1)}, f32[24,128]{1,0:T(8,128)S(1)}, u32[]{:S(2)}, u32[]{:S(2)}) collective-permute-start(f32[24,128]{1,0:T(8,128)S(1)} %get-tuple-element.23.own_high), channel_id=1, source_target_pairs={{0,1},{1,2},{2,3},{3,0},{4,5},{5,6},{6,7},{7,4},{8,9},{9,10},{10,1... | collective-permute-start | bytes 36872 | tf_op jit(solution)/shard_map/ppermute | solution.py:393
  18.8 3.9 %collective-permute-start.6 = (f32[24,128]{1,0:T(8,128)S(1)}, f32[24,128]{1,0:T(8,128)S(1)}, u32[]{:S(2)}, u32[]{:S(2)}) collective-permute-start(f32[24,128]{1,0:T(8,128)S(1)} %get-tuple-element.24.own_low), channel_id=1, source_target_pairs={{0,3},{1,0},{2,1},{3,2},{4,7},{5,4},{6,5},{7,6},{8,11},{9,8},{10,9... | collective-permute-start | bytes 36872 | tf_op jit(solution)/shard_map/ppermute | solution.py:393

commit v2 on v0

--- a/solution.py
+++ b/solution.py
@@ -252,6 +252,12 @@
     tall = (ny + 8, nz)
     lane = lanes(tall)
 
+    def pairs(low, high, shape):
+        is_even, high = lanes(shape) % 2 == 0, roll(high, -1, 1)
+        return jnp.where(is_even, low, high), jnp.where(is_even, high, low)
+
+    beyond = pairs(z_lo, z_hi, tall)
+
     def signed(k, x):
         if x < 0:
             main = from_below[k if x == -1 else 10 + k]
@@ -265,8 +271,9 @@
         at = (k, x + 2)
         a = jnp.abs(signed(k, x))
         column = k * wide + x + 2
-        minus = jnp.where(lane == 0, jnp.abs(roll(z_lo, -column, 1)), roll(a, 1, 1))
-        plus = jnp.where(lane == nz - 1, jnp.abs(roll(z_hi, nz - 1 - column, 1)), roll(a, -1, 1))
+        outer = jnp.abs(roll(beyond[column % 2], -column, 1))
+        minus = jnp.where(lane == 0, outer, roll(a, 1, 1))
+        plus = jnp.where(lane == nz - 1, outer, roll(a, -1, 1))
         z_sum, dz = plus + minus, plus - minus
         store_rows(a_ref, at, a[:ny], a[ny:])
         a_up, a_down = load_rows(a_ref, at, 1, ny), load_rows(a_ref, at, -1, ny)

time: 24.8 us -> 24.8 us (level)
  no operation moved by 1% of the time
where the time goes in v2:
time: 24.8 us; the launch traced here: 24.7 us
  starting transfers between devices  10.9 us (44%)
  waiting for transfers between devices  9.94 us (40%)
  Pallas kernels  3.78 us (15%)
    ppermute x8, starting transfers between devices, ring(): lax.ppermute(value, axis, [(i, (i + step) % count) for i in range(count)])  10.9 us
    ppermute x8, waiting for transfers between devices, ring(): lax.ppermute(value, axis, [(i, (i + step) % count) for i in range(count)])  9.94 us
    pallas_call x6, Pallas kernels, call(): pl.pallas_call(kernel, out_shape=[jax.ShapeDtypeStruct(*(s if isinstance(...  3.78 us
  transfers between devices with their start and end apart: 8, of which 6 were waited for; matrix products, arithmetic and copies ran while one was open for 0% of the time, Pallas kernels for 1%

profile of v2, /device:TPU:0, one launch (start us, length us, event | category | flops | bytes accessed | tf_op | source)
XLA Modules:
  0.0 24.7 jit_solution(16390442216304918625)
XLA Ops:
  0.0 1.4 %shard_map.28 = (f32[5,4,16,128]{3,2,1,0:T(8,128)S(1)}, f32[12,16,128]{2,1,0:T(8,128)S(1)}, f32[12,16,128]{2,1,0:T(8,128)S(1)}, f32[16,128]{1,0:T(8,128)S(1)}, f...) custom-call(f32[2,19,4,16,128]{4,3,2,1,0:T(8,128)} %pop_hbm.1, ...), custom_call_target="tpu_custom_call" | custom-call | flops 200000 | bytes 200000 | tf_op jit(solution)/shard_map/pallas_call | solution.py:411
  1.5 3.0 %collective-permute-start.3 = (f32[12,16,128]{2,1,0:T(8,128)S(1)}, f32[12,16,128]{2,1,0:T(8,128)S(1)}, u32[]{:S(2)}, u32[]{:S(2)}) collective-permute-start(f32[12,16,128]{2,1,0:T(8,128)S(1)} %get-tuple-element.25), channel_id=1, source_target_pairs={{0,8},{8,16},{16,24},{24,0},{1,9},{9,17},{17,25},{25,1},{2,10},{10... | collective-permute-start | bytes 294920 | tf_op jit(solution)/shard_map/ppermute | solution.py:397
  4.5 1.0 %collective-permute-start.4 = (f32[12,16,128]{2,1,0:T(8,128)S(1)}, f32[12,16,128]{2,1,0:T(8,128)S(1)}, u32[]{:S(2)}, u32[]{:S(2)}) collective-permute-start(f32[12,16,128]{2,1,0:T(8,128)S(1)} %get-tuple-element.26), channel_id=1, source_target_pairs={{0,24},{8,0},{16,8},{24,16},{1,25},{9,1},{17,9},{25,17},{2,26},{10... | collective-permute-start | bytes 294920 | tf_op jit(solution)/shard_map/ppermute | solution.py:397
  5.5 3.4 %collective-permute-done.3.from_below = f32[12,16,128]{2,1,0:T(8,128)S(1)} collective-permute-done((f32[12,16,128]{2,1,0:T(8,128)S(1)}, f32[12,16,128]{2,1,0:T(8,128)S(1)}, u32[]{:S(2)}, u32[]{:S(2)}) %collective-permute-start.3) | collective-permute-done | bytes 98336 | tf_op jit(solution)/shard_map/ppermute | solution.py:397
  8.9 1.7 %collective-permute-done.4.from_above = f32[12,16,128]{2,1,0:T(8,128)S(1)} collective-permute-done((f32[12,16,128]{2,1,0:T(8,128)S(1)}, f32[12,16,128]{2,1,0:T(8,128)S(1)}, u32[]{:S(2)}, u32[]{:S(2)}) %collective-permute-start.4) | collective-permute-done | bytes 98336 | tf_op jit(solution)/shard_map/ppermute | solution.py:397
  10.6 0.1 collective-permute-start.7
  10.7 1.6 %collective-permute-start = (f32[16,128]{1,0:T(8,128)S(1)}, f32[16,128]{1,0:T(8,128)S(1)}, u32[]{:S(2)}, u32[]{:S(2)}) collective-permute-start(f32[16,128]{1,0:T(8,128)S(1)} %get-tuple-element.19), channel_id=1, source_target_pairs={{0,8},{8,16},{16,24},{24,0},{1,9},{9,17},{17,25},{25,1},{2,10},{10... | collective-permute-start | bytes 24584 | tf_op jit(solution)/shard_map/ppermute | solution.py:397
  12.3 1.4 %collective-permute-start.1 = (f32[16,128]{1,0:T(8,128)S(1)}, f32[16,128]{1,0:T(8,128)S(1)}, u32[]{:S(2)}, u32[]{:S(2)}) collective-permute-start(f32[16,128]{1,0:T(8,128)S(1)} %get-tuple-element.20), channel_id=1, source_target_pairs={{0,24},{8,0},{16,8},{24,16},{1,25},{9,1},{17,9},{25,17},{2,26},{10... | collective-permute-start | bytes 24584 | tf_op jit(solution)/shard_map/ppermute | solution.py:397
  13.7 0.3 %shard_map.29.sheets = f32[2,16,128]{2,1,0:T(8,128)S(1)} custom-call(f32[5,4,16,128]{3,2,1,0:T(8,128)S(1)} %get-tuple-element.18.field, f32[2,19,4,16,128]{4,3,2,1,0:T(8,128)S(1)} %get-tuple-element.16.pop), custom_call_target="tpu_custom_call" | custom-call | flops 200000 | bytes 200000 | tf_op jit(solution)/shard_map/pallas_call | solution.py:411
  13.9 1.4 %collective-permute-done.from_below = f32[16,128]{1,0:T(8,128)S(1)} collective-permute-done((f32[16,128]{1,0:T(8,128)S(1)}, f32[16,128]{1,0:T(8,128)S(1)}, u32[]{:S(2)}, u32[]{:S(2)}) %collective-permute-start) | collective-permute-done | bytes 8224 | tf_op jit(solution)/shard_map/ppermute | solution.py:397
  15.3 0.7 %collective-permute-done.1.from_above = f32[16,128]{1,0:T(8,128)S(1)} collective-permute-done((f32[16,128]{1,0:T(8,128)S(1)}, f32[16,128]{1,0:T(8,128)S(1)}, u32[]{:S(2)}, u32[]{:S(2)}) %collective-permute-start.1) | collective-permute-done | bytes 8224 | tf_op jit(solution)/shard_map/ppermute | solution.py:397
  16.0 0.1 shard_map.30
  16.0 0.0 collective-permute-start.2
  16.1 1.2 %collective-permute-done.2.rest_0_ = f32[2,8,128]{2,1,0:T(8,128)S(1)} collective-permute-done((f32[2,8,128]{2,1,0:T(8,128)S(1)}, f32[2,8,128]{2,1,0:T(8,128)S(1)}, u32[]{:S(2)}, u32[]{:S(2)}) %collective-permute-start.2) | collective-permute-done | bytes 8224 | tf_op jit(solution)/shard_map/ppermute | solution.py:397
  17.2 1.6 %collective-permute-start.5 = (f32[24,128]{1,0:T(8,128)S(1)}, f32[24,128]{1,0:T(8,128)S(1)}, u32[]{:S(2)}, u32[]{:S(2)}) collective-permute-start(f32[24,128]{1,0:T(8,128)S(1)} %get-tuple-element.23.own_high), channel_id=1, source_target_pairs={{0,1},{1,2},{2,3},{3,0},{4,5},{5,6},{6,7},{7,4},{8,9},{9,10},{10,1... | collective-permute-start | bytes 36872 | tf_op jit(solution)/shard_map/ppermute | solution.py:397
  18.8 2.2 %collective-permute-start.6 = (f32[24,128]{1,0:T(8,128)S(1)}, f32[24,128]{1,0:T(8,128)S(1)}, u32[]{:S(2)}, u32[]{:S(2)}) collective-permute-start(f32[24,128]{1,0:T(8,128)S(1)} %get-tuple-element.24.own_low), channel_id=1, source_target_pairs={{0,3},{1,0},{2,1},{3,2},{4,7},{5,4},{6,5},{7,6},{8,11},{9,8},{10,9... | collective-permute-start | bytes 36872 | tf_op jit(solution)/shard_map/ppermute | solution.py:397
  21.1 1.7 %collective-permute-done.5.z_low = f32[24,128]{1,0:T(8,128)S(1)} collective-permute-done((f32[24,128]{1,0:T(8,128)S(1)}, f32[24,128]{1,0:T(8,128)S(1)}, u32[]{:S(2)}, u32[]{:S(2)}) %collective-permute-start.5) | collective-permute-done | bytes 12320 | tf_op jit(solution)/shard_map/ppermute | solution.py:397
  22.7 0.0 collective-permute-done.6.z_high
  22.7 0.0 collective-permute-done.7.rest_0_
  22.7 2.0 %shard_map.33 = f32[2,19,4,16,128]{4,3,2,1,0:T(8,128)} custom-call(f32[2,19,4,16,128]{4,3,2,1,0:T(8,128)S(1)} %get-tuple-element.16.pop, s32[4,16,128]{2,1,0:T(8,128)S(1)} %get-tuple-element.17.solid, f32[5,4,16,128]{3,2,1,0:T(8,128)S(1)} %get-tuple-element.18.field, f32[24,128]{1,0:T(8,128)S(1)} %get-tuple-element.23.own_high, ...), custom_call_target="tpu_custom_call" | custom-call | flops 200000 | bytes 200000 | tf_op jit(solution)/shard_map/pallas_call | solution.py:411
  (2 shorter events, 0.0 us)
Async XLA Ops:
  1.5 7.4 %collective-permute-start.3 = (f32[12,16,128]{2,1,0:T(8,128)S(1)}, f32[12,16,128]{2,1,0:T(8,128)S(1)}, u32[]{:S(2)}, u32[]{:S(2)}) collective-permute-start(f32[12,16,128]{2,1,0:T(8,128)S(1)} %get-tuple-element.25), channel_id=1, source_target_pairs={{0,8},{8,16},{16,24},{24,0},{1,9},{9,17},{17,25},{25,1},{2,10},{10... | collective-permute-start | bytes 294920 | tf_op jit(solution)/shard_map/ppermute | solution.py:397
  4.5 6.1 %collective-permute-start.4 = (f32[12,16,128]{2,1,0:T(8,128)S(1)}, f32[12,16,128]{2,1,0:T(8,128)S(1)}, u32[]{:S(2)}, u32[]{:S(2)}) collective-permute-start(f32[12,16,128]{2,1,0:T(8,128)S(1)} %get-tuple-element.26), channel_id=1, source_target_pairs={{0,24},{8,0},{16,8},{24,16},{1,25},{9,1},{17,9},{25,17},{2,26},{10... | collective-permute-start | bytes 294920 | tf_op jit(solution)/shard_map/ppermute | solution.py:397
  10.6 12.1 %collective-permute-start.7 = (f32[56,8,128]{2,1,0:T(8,128)S(1)}, f32[56,8,128]{2,1,0:T(8,128)S(1)}, u32[]{:S(2)}, u32[]{:S(2)}) collective-permute-start(f32[56,8,128]{2,1,0:T(8,128)S(1)} %shard_map.32), channel_id=1, source_target_pairs={{0,4},{4,0},{1,5},{5,1},{2,6},{6,2},{3,7},{7,3},{8,12},{12,8},{9,1... | collective-permute-start | bytes 688136 | tf_op jit(solution)/shard_map/ppermute | solution.py:397
  10.7 4.6 %collective-permute-start = (f32[16,128]{1,0:T(8,128)S(1)}, f32[16,128]{1,0:T(8,128)S(1)}, u32[]{:S(2)}, u32[]{:S(2)}) collective-permute-start(f32[16,128]{1,0:T(8,128)S(1)} %get-tuple-element.19), channel_id=1, source_target_pairs={{0,8},{8,16},{16,24},{24,0},{1,9},{9,17},{17,25},{25,1},{2,10},{10... | collective-permute-start | bytes 24584 | tf_op jit(solution)/shard_map/ppermute | solution.py:397
  12.3 3.7 %collective-permute-start.1 = (f32[16,128]{1,0:T(8,128)S(1)}, f32[16,128]{1,0:T(8,128)S(1)}, u32[]{:S(2)}, u32[]{:S(2)}) collective-permute-start(f32[16,128]{1,0:T(8,128)S(1)} %get-tuple-element.20), channel_id=1, source_target_pairs={{0,24},{8,0},{16,8},{24,16},{1,25},{9,1},{17,9},{25,17},{2,26},{10... | collective-permute-start | bytes 24584 | tf_op jit(solution)/shard_map/ppermute | solution.py:397
  16.0 1.2 %collective-permute-start.2 = (f32[2,8,128]{2,1,0:T(8,128)S(1)}, f32[2,8,128]{2,1,0:T(8,128)S(1)}, u32[]{:S(2)}, u32[]{:S(2)}) collective-permute-start(f32[2,8,128]{2,1,0:T(8,128)S(1)} %get-tuple-element.22), channel_id=1, source_target_pairs={{0,4},{4,0},{1,5},{5,1},{2,6},{6,2},{3,7},{7,3},{8,12},{12,8},{9,1... | collective-permute-start | bytes 24584 | tf_op jit(solution)/shard_map/ppermute | solution.py:397
  17.2 5.5 %collective-permute-start.5 = (f32[24,128]{1,0:T(8,128)S(1)}, f32[24,128]{1,0:T(8,128)S(1)}, u32[]{:S(2)}, u32[]{:S(2)}) collective-permute-start(f32[24,128]{1,0:T(8,128)S(1)} %get-tuple-element.23.own_high), channel_id=1, source_target_pairs={{0,1},{1,2},{2,3},{3,0},{4,5},{5,6},{6,7},{7,4},{8,9},{9,10},{10,1... | collective-permute-start | bytes 36872 | tf_op jit(solution)/shard_map/ppermute | solution.py:397
  18.8 3.9 %collective-permute-start.6 = (f32[24,128]{1,0:T(8,128)S(1)}, f32[24,128]{1,0:T(8,128)S(1)}, u32[]{:S(2)}, u32[]{:S(2)}) collective-permute-start(f32[24,128]{1,0:T(8,128)S(1)} %get-tuple-element.24.own_low), channel_id=1, source_target_pairs={{0,3},{1,0},{2,1},{3,2},{4,7},{5,4},{6,5},{7,6},{8,11},{9,8},{10,9... | collective-permute-start | bytes 36872 | tf_op jit(solution)/shard_map/ppermute | solution.py:397
